TPU v7x, 32 devices: a whole 2x2x4 slice. The times are simulated.
32 devices in a mesh: tok: 8 (over z, x), exp: 4 (over y, core).
Axes of the slice: x: 2, y: 2, z: 4, core: 2. Of those that a mesh axis runs over, the one named last changes fastest.
Arguments:
- tokens: bfloat16 [16384, 7168], P('tok', 'exp'), may hold values from -6 to 6
- gate_weight: bfloat16 [7168, 256], P('exp'), may hold values from -0.0625 to 0.0625
- expert_ids: int32 [16384, 8], P('tok'), may hold values from 0 to 255, all different within a row
- expert_bias: float32 [256], P('exp'), may hold values from -0.002 to 0.002
Outputs:
- affinities: float32 [16384, 256], P('tok', 'exp')
- weights: float32 [16384, 8], P('tok')
- load: float32 [256], replicated
- new_bias: float32 [256], replicated
All inputs are finite; a program needn't handle non-finite values.
Results may differ from a plain program's by a relative error of at most 0.0003.
Values may be sent and summed in bfloat16 or wider, within the bound.
No kernel may reach another device: no remote copies, remote signals or barrier semaphores. Data moves between devices by JAX's collectives and lax.ppermute only.
A program may use at most 64 MiB of HBM per device.

v0:
```python
import jax
import jax.numpy as jnp
from jax import lax
from jax.sharding import PartitionSpec as P


def count_experts(expert_ids, width):
    numbers = lax.iota(jnp.int32, width)
    matches = expert_ids[:, :, None] == numbers[None, None, :]
    return jnp.sum(matches.astype(jnp.float32), axis=(0, 1))


def local(tokens, gate_weight, expert_ids, expert_bias):
    experts_all = gate_weight.shape[1]
    own_width = expert_bias.shape[0]
    first_expert = lax.axis_index("exp") * own_width
    tok_rows = tokens.shape[0]
    partial_logits = jnp.dot(tokens, gate_weight, preferred_element_type=jnp.float32)
    logits = lax.psum_scatter(partial_logits, "exp", scatter_dimension=1, tiled=True)
    affinities = jax.nn.sigmoid(logits)
    numbers = first_expert + lax.iota(jnp.int32, own_width)
    matches = expert_ids[:, :, None] == numbers[None, None, :]
    chosen_part = jnp.sum(jnp.where(matches, affinities[:, None, :], jnp.float32(0.0)), axis=2)
    chosen = lax.psum(chosen_part, "exp")
    weights = 2.5 * chosen / jnp.sum(chosen, axis=1, keepdims=True)
    target = jnp.float32(tok_rows * lax.axis_size("tok") * expert_ids.shape[1])
    bias_whole = lax.all_gather(expert_bias, "exp", axis=0, tiled=True)
    load = lax.psum(count_experts(expert_ids, experts_all), "tok")
    new_bias = bias_whole + 0.001 * jnp.sign(target - jnp.float32(experts_all) * load)
    return (affinities, weights, load, new_bias)


def solution(mesh):
    in_specs = (P("tok", "exp"), P("exp", None), P("tok", None), P("exp"))
    out_specs = (P("tok", "exp"), P("tok", None), P(), P())
    return jax.shard_map(local, mesh=mesh, in_specs=in_specs, out_specs=out_specs, check_vma=False)
```

profile of v0, /device:TPU:0, one launch (start us, length us, event | category | flops | bytes accessed | tf_op | source)
XLA Modules:
  0.0 92.7 jit_solution(2102868022089184914)
XLA Ops:
  7.2 0.0 copy-start
  7.2 0.0 copy-start.5
  7.2 0.0 copy-start.2
  7.2 0.0 copy-start.4
  7.2 0.0 reduce-scatter.2.cloned.1.call-start
  7.3 1.1 %copy-done = bf16[1792,256]{1,0:T(8,128)(2,1)S(1)} copy-done((bf16[1792,256]{1,0:T(8,128)(2,1)S(1)}, bf16[1792,256]{1,0:T(8,128)(2,1)}, u32[]{:S(2)}) %copy-start) | copy-done | bytes 917528
  8.4 6.5 %fusion = f32[2048,256]{0,1:T(8,128)} fusion(bf16[2048,1792]{1,0:T(8,128)(2,1)} %param.4, bf16[1792,256]{1,0:T(8,128)(2,1)S(1)} %copy-done), kind=kOutput, calls=%fused_computation.7 | convolution fusion | flops 1879048192 | bytes 10354688 | tf_op jit(solution)/shard_map/dot_general | solution.py:18
  14.9 0.0 reduce-scatter.2.cloned.1.call-update
  14.9 0.0 all-reduce.3.cloned.1.call-start
  15.0 0.0 copy-done.2
  15.0 0.3 copy.11
  15.4 0.0 copy-done.5
  15.4 0.6 dynamic-slice
  16.6 0.0 copy-done.4
  16.6 0.2 dynamic-update-slice
  16.9 5.1 %convert_reduce_fusion = f32[256]{0:T(256)S(1)} fusion(s32[2048,8]{1,0:T(8,128)S(1)} %copy.11), kind=kLoop, calls=%fused_computation | loop fusion | flops 12582656 | bytes 66560 | tf_op jit(solution)/shard_map/reduce_sum | solution.py:10
  22.0 23.1 %psum.15 = f32[256]{0:T(256)S(1)} all-reduce(f32[256]{0:T(256)S(1)} %convert_reduce_fusion), channel_id=1, replica_groups=mesh['tok'=8,'exp'=4] {'tok'}, use_global_device_ids=true, to_apply=%region_5.6 | all-reduce | flops 256 | bytes 2048 | tf_op jit(solution)/shard_map/psum | solution.py:28
  45.1 0.0 copy-start.3
  45.1 5.7 %all-reduce = f32[256]{0:T(256)S(1)} all-reduce(f32[256]{0:T(256)S(1)} %dynamic-update-slice), channel_id=1, replica_groups=mesh['tok'=8,'exp'=4] {'exp'}, use_global_device_ids=true, to_apply=%add | all-reduce | flops 256 | bytes 2048
  50.8 0.0 reduce-scatter.2.cloned.1.call-done
  50.8 1.2 %add_divide_fusion = f32[2048,64]{0,1:T(8,128)S(1)} fusion(f32[2048,64]{0,1:T(8,128)} %reduce-scatter.2.cloned.1.call-done), kind=kLoop, calls=%fused_computation.3 | loop fusion | flops 393216 | bytes 1048576 | tf_op jit(solution)/shard_map/div | solution.py:20
  52.0 0.0 copy-start.1
  52.0 1.2 %select_reduce_fusion = f32[2048,8]{0,1:T(8,128)} fusion(f32[2048,64]{0,1:T(8,128)S(1)} %add_divide_fusion, s32[2048,8]{0,1:T(8,128)S(1)} %copy-done.2, s32[64]{0:T(128)S(1)} %iota_add_fusion), kind=kLoop, calls=%fused_computation.2 | loop fusion | flops 3129344 | bytes 655616 | tf_op jit(solution)/shard_map/reduce_sum | solution.py:23
  53.2 0.0 all-reduce.3.cloned.1.call-update
  53.2 0.6 multiply_add_fusion
  53.8 29.7 %all-reduce.3.cloned.1.call-done = f32[2048,8]{0,1:T(8,128)} async-done(((f32[2048,8]{0,1:T(8,128)}), f32[2048,8]{0,1:T(8,128)}) %all-reduce.3.cloned.1.call-update) | async-done | bytes 65552 | tf_op jit(solution)/shard_map/psum | solution.py:24
  83.5 0.9 reduce_sum.28
  84.4 1.5 %multiply_divide_fusion = f32[2048,8]{0,1:T(8,128)} fusion(f32[2048,8]{0,1:T(8,128)} %all-reduce.3.cloned.1.call-done, f32[2048]{0:T(1024)S(1)} %reduce_sum.28), kind=kLoop, calls=%fused_computation.4 | loop fusion | flops 32768 | bytes 139264 | tf_op jit(solution)/shard_map/div | solution.py:25
  85.9 0.0 copy-done.3
  85.9 0.0 copy-done.1
  (2 shorter events, 0.0 us)
Async XLA Ops:
  7.2 1.2 %copy-start = (bf16[1792,256]{1,0:T(8,128)(2,1)S(1)}, bf16[1792,256]{1,0:T(8,128)(2,1)}, u32[]{:S(2)}) copy-start(bf16[1792,256]{1,0:T(8,128)(2,1)} %param.5) | copy-start | bytes 2752516
  7.2 8.2 %copy-start.5 = (u32[32]{0:T(128)S(1)}, u32[32]{0:T(128)}, u32[]{:S(2)}) copy-start(u32[32]{0:T(128)} %constant.20) | copy-start | bytes 388
  7.2 7.8 %copy-start.2 = (s32[2048,8]{0,1:T(8,128)S(1)}, s32[2048,8]{0,1:T(8,128)}, u32[]{:S(2)}) copy-start(s32[2048,8]{0,1:T(8,128)} %param.6) | copy-start | bytes 196612
  7.2 9.4 %copy-start.4 = (f32[64]{0:T(128)S(1)}, f32[64]{0:T(128)}, u32[]{:S(2)}) copy-start(f32[64]{0:T(128)} %param.7) | copy-start | bytes 772
  7.2 43.6 %reduce-scatter.2.cloned.1.call-start = ((), (), s32[]{:S(2)}) async-start(), calls=%async_computation.1 | async-start | bytes 2621440 | tf_op jit(solution)/shard_map/reduce_scatter | solution.py:19
  14.9 68.6 %all-reduce.3.cloned.1.call-start = ((), (), s32[]{:S(2)}) async-start(), calls=%async_computation.2 | async-start | bytes 131072 | tf_op jit(solution)/shard_map/psum | solution.py:24
  45.1 40.8 %copy-start.3 = (f32[256]{0:T(256)}, f32[256]{0:T(256)S(1)}, u32[]{:S(2)}) copy-start(f32[256]{0:T(256)S(1)} %psum.15) | copy-start | bytes 3076
  52.0 33.9 %copy-start.1 = (f32[2048,64]{0,1:T(8,128)}, f32[2048,64]{0,1:T(8,128)S(1)}, u32[]{:S(2)}) copy-start(f32[2048,64]{0,1:T(8,128)S(1)} %add_divide_fusion) | copy-start | bytes 1572868
Sparse Core Ops, SparseCore 0:
  15.1 33.8 reduce-scatter.1
  53.3 30.1 all-reduce.2
where the time goes:
time: 93.1 us; the launch traced here: 92.7 us
  waiting for transfers between devices  29.8 us (32%)
  blocking collectives  28.8 us (31%)
  between operations  14.8 us (16%)
  other arithmetic  10.4 us (11%)
  matrix products  6.53 us (7%)
  local copies, waits for them, and re-layouts  2.31 us (2%)
    psum x1, waiting for transfers between devices, local(): chosen = lax.psum(chosen_part, 'exp')  29.7 us
    psum x1, blocking collectives, local(): load = lax.psum(count_experts(expert_ids, experts_all), 'tok')  23.1 us
    dot_general x1, matrix products, local(): jnp.dot(tokens, gate_weight, preferred_element_type=jnp.float32)  6.53 us
    unnamed x1, blocking collectives  5.66 us
    reduce_sum x1, other arithmetic, count_experts(): return jnp.sum(matches.astype(jnp.float32), axis=(0, 1))  5.11 us
    unnamed x16, local copies, waits for them, and re-layouts  2.31 us
  transfers between devices with their start and end apart: 2, of which 1 were waited for; matrix products, arithmetic and copies ran while one was open for 7% of the time, Pallas kernels for 0%

commit v1 on v0

--- a/solution.py
+++ b/solution.py
@@ -21,7 +21,7 @@
     numbers = first_expert + lax.iota(jnp.int32, own_width)
     matches = expert_ids[:, :, None] == numbers[None, None, :]
     chosen_part = jnp.sum(jnp.where(matches, affinities[:, None, :], jnp.float32(0.0)), axis=2)
-    chosen = lax.psum(chosen_part, "exp")
+    chosen = jnp.sum(lax.all_gather(chosen_part, "exp"), axis=0)
     weights = 2.5 * chosen / jnp.sum(chosen, axis=1, keepdims=True)
     target = jnp.float32(tok_rows * lax.axis_size("tok") * expert_ids.shape[1])
     bias_whole = lax.all_gather(expert_bias, "exp", axis=0, tiled=True)

time: 93.1 us -> 67 us (0.72)
  waiting for transfers between devices: 29.8 us -> 0.02 us
  blocking collectives: 28.8 us -> 34.8 us
  other arithmetic: 10.4 us -> 8.2 us
    psum x1 -> x0, waiting for transfers between devices: 29.7 us -> none  [local(): chosen = lax.psum(chosen_part, 'exp')]
    all_gather x0 -> x1, blocking collectives: none -> 5.99 us  [local(): chosen = jnp.sum(lax.all_gather(chosen_part, 'exp'), axis=0)]
  transfers between devices with their start and end apart: 2 -> 1, of which waited for: 1 -> 0; matrix products, arithmetic and copies ran while one was open for 7% -> 10% of each run, Pallas kernels for 0% -> 0%
where the time goes in v1:
time: 67 us; the launch traced here: 66.7 us
  blocking collectives  34.8 us (52%)
  between operations  14.8 us (22%)
  other arithmetic  8.2 us (12%)
  matrix products  6.53 us (10%)
  local copies, waits for them, and re-layouts  2.33 us (3%)
    psum x1, blocking collectives, local(): load = lax.psum(count_experts(expert_ids, experts_all), 'tok')  23.1 us
    dot_general x1, matrix products, local(): jnp.dot(tokens, gate_weight, preferred_element_type=jnp.float32)  6.53 us
    all_gather x1, blocking collectives, local(): chosen = jnp.sum(lax.all_gather(chosen_part, 'exp'), axis=0)  5.99 us
    unnamed x1, blocking collectives  5.66 us
    reduce_sum x1, other arithmetic, count_experts(): return jnp.sum(matches.astype(jnp.float32), axis=(0, 1))  5.11 us
    unnamed x16, local copies, waits for them, and re-layouts  2.31 us
  transfers between devices with their start and end apart: 1, of which 0 were waited for; matrix products, arithmetic and copies ran while one was open for 10% of the time, Pallas kernels for 0%

profile of v1, /device:TPU:0, one launch (start us, length us, event | category | flops | bytes accessed | tf_op | source)
XLA Modules:
  0.0 66.7 jit_solution(8480631813736376254)
XLA Ops:
  7.2 0.0 copy-start
  7.2 0.0 copy-start.5
  7.2 0.0 copy-start.2
  7.2 0.0 copy-start.4
  7.2 0.0 reduce-scatter.2.cloned.1.call-start
  7.3 1.1 %copy-done = bf16[1792,256]{1,0:T(8,128)(2,1)S(1)} copy-done((bf16[1792,256]{1,0:T(8,128)(2,1)S(1)}, bf16[1792,256]{1,0:T(8,128)(2,1)}, u32[]{:S(2)}) %copy-start) | copy-done | bytes 917528
  8.4 6.5 %fusion = f32[2048,256]{0,1:T(8,128)} fusion(bf16[2048,1792]{1,0:T(8,128)(2,1)} %param.4, bf16[1792,256]{1,0:T(8,128)(2,1)S(1)} %copy-done), kind=kOutput, calls=%fused_computation.7 | convolution fusion | flops 1879048192 | bytes 10354688 | tf_op jit(solution)/shard_map/dot_general | solution.py:18
  14.9 0.0 reduce-scatter.2.cloned.1.call-update
  14.9 0.0 copy-done.2
  15.0 0.3 copy.11
  15.3 0.0 copy-done.5
  15.3 0.6 dynamic-slice
  16.6 0.0 copy-done.4
  16.6 0.2 dynamic-update-slice
  16.8 5.1 %convert_reduce_fusion = f32[256]{0:T(256)S(1)} fusion(s32[2048,8]{1,0:T(8,128)S(1)} %copy.11), kind=kLoop, calls=%fused_computation | loop fusion | flops 12582656 | bytes 66560 | tf_op jit(solution)/shard_map/reduce_sum | solution.py:10
  21.9 23.1 %psum.7 = f32[256]{0:T(256)S(1)} all-reduce(f32[256]{0:T(256)S(1)} %convert_reduce_fusion), channel_id=1, replica_groups=mesh['tok'=8,'exp'=4] {'tok'}, use_global_device_ids=true, to_apply=%region_5.6 | all-reduce | flops 256 | bytes 2048 | tf_op jit(solution)/shard_map/psum | solution.py:28
  45.0 0.0 copy-start.3
  45.0 5.7 %all-reduce = f32[256]{0:T(256)S(1)} all-reduce(f32[256]{0:T(256)S(1)} %dynamic-update-slice), channel_id=1, replica_groups=mesh['tok'=8,'exp'=4] {'exp'}, use_global_device_ids=true, to_apply=%add | all-reduce | flops 256 | bytes 2048
  50.7 0.6 multiply_add_fusion
  51.3 0.0 reduce-scatter.2.cloned.1.call-done
  51.3 1.2 %add_divide_fusion = f32[2048,64]{0,1:T(8,128)S(1)} fusion(f32[2048,64]{0,1:T(8,128)} %reduce-scatter.2.cloned.1.call-done), kind=kLoop, calls=%fused_computation.3 | loop fusion | flops 393216 | bytes 1048576 | tf_op jit(solution)/shard_map/div | solution.py:20
  52.5 0.0 copy-start.1
  52.5 0.6 select_reduce_fusion
  53.1 6.0 %all-gather = f32[8192,8]{0,1:T(8,128)S(1)} all-gather(f32[2048,8]{0,1:T(8,128)S(1)} %select_reduce_fusion), channel_id=2, replica_groups=mesh['tok'=8,'exp'=4] {'exp'}, dimensions={0}, use_global_device_ids=true | all-gather | bytes 327680 | tf_op jit(solution)/shard_map/all_gather | solution.py:24
  59.1 0.1 reduce.1
  59.2 0.6 multiply_divide_fusion
  59.9 0.0 copy-done.3
  59.9 0.0 copy-done.1
  (5 shorter events, 0.1 us)
Async XLA Ops:
  7.2 1.2 %copy-start = (bf16[1792,256]{1,0:T(8,128)(2,1)S(1)}, bf16[1792,256]{1,0:T(8,128)(2,1)}, u32[]{:S(2)}) copy-start(bf16[1792,256]{1,0:T(8,128)(2,1)} %param.5) | copy-start | bytes 2752516
  7.2 8.1 %copy-start.5 = (u32[32]{0:T(128)S(1)}, u32[32]{0:T(128)}, u32[]{:S(2)}) copy-start(u32[32]{0:T(128)} %constant.20) | copy-start | bytes 388
  7.2 7.8 %copy-start.2 = (s32[2048,8]{0,1:T(8,128)S(1)}, s32[2048,8]{0,1:T(8,128)}, u32[]{:S(2)}) copy-start(s32[2048,8]{0,1:T(8,128)} %param.6) | copy-start | bytes 196612
  7.2 9.4 %copy-start.4 = (f32[64]{0:T(128)S(1)}, f32[64]{0:T(128)}, u32[]{:S(2)}) copy-start(f32[64]{0:T(128)} %param.7) | copy-start | bytes 772
  7.2 44.1 %reduce-scatter.2.cloned.1.call-start = ((), (), s32[]{:S(2)}) async-start(), calls=%async_computation.1 | async-start | bytes 2621440 | tf_op jit(solution)/shard_map/reduce_scatter | solution.py:19
  45.0 14.8 %copy-start.3 = (f32[256]{0:T(256)}, f32[256]{0:T(256)S(1)}, u32[]{:S(2)}) copy-start(f32[256]{0:T(256)S(1)} %psum.7) | copy-start | bytes 3076
  52.5 7.4 %copy-start.1 = (f32[2048,64]{0,1:T(8,128)}, f32[2048,64]{0,1:T(8,128)S(1)}, u32[]{:S(2)}) copy-start(f32[2048,64]{0,1:T(8,128)S(1)} %add_divide_fusion) | copy-start | bytes 1572868
Sparse Core Ops, SparseCore 0:
  15.1 33.9 reduce-scatter.1
